TPU v7x, 32 devices: a whole 2x2x4 slice. The times are simulated.
32 devices in a mesh: dp: 2 (over x), x: 4 (over z), y: 4 (over y, core).
Axes of the slice: x: 2, y: 2, z: 4, core: 2. Of those that a mesh axis runs over, the one named last changes fastest.
Arguments:
- hidden: bfloat16 [2048, 1024], P('dp', 'x'), parts along dimension 0
- w_qkv: bfloat16 [1024, 3072], P('x', 'y')
- b_qkv: bfloat16 [3072], P('y')
- w_out: bfloat16 [1024, 1024], P('y', 'x')
- b_out: bfloat16 [1024], P('x')
- attn_gain: bfloat16 [1024], P('x')
- attn_shift: bfloat16 [1024], P('x')
- w_up: bfloat16 [1024, 2, 4096], P('x', None, 'y')
- b_up: bfloat16 [2, 4096], P(None, 'y')
- w_down: bfloat16 [4096, 1024], P('y', 'x')
- b_down: bfloat16 [1024], P('x')
- mlp_gain: bfloat16 [1024], P('x')
- mlp_shift: bfloat16 [1024], P('x')
- k_cache: bfloat16 [2048, 64, 16, 64], P('dp', None, 'y'), parts along dimension 0
- v_cache: bfloat16 [2048, 64, 16, 64], P('dp', None, 'y'), parts along dimension 0
- positions: int32 [2048], P('dp'), parts along dimension 0
- lengths: int32 [2048], P('dp'), parts along dimension 0
Outputs:
- output 1: bfloat16 [2048, 1024], P('dp', 'x'), parts along dimension 0
- output 2: bfloat16 [2048, 64, 16, 64], P('dp', None, 'y'), parts along dimension 0
- output 3: bfloat16 [2048, 64, 16, 64], P('dp', None, 'y'), parts along dimension 0
There are 2 independent parts. A program takes and returns all parts, laid end to end along the dimension named above; an argument that names none is the same for every part.
All inputs are finite; a program needn't handle non-finite values.
Results may differ from a plain program's by a relative error of at most 0.02.
Values are sent between devices in bfloat16 or wider.
A program may use at most 1 GiB of HBM per device.

v0:
```python
import math
import jax
import jax.numpy as jnp
from jax import lax
from jax.sharding import PartitionSpec as P

DEEP_ALPHA = math.sqrt(140.0)
LN_EPS = 1e-5
ROPE_BASE = 10000.0


def apply_rotary(head_vec, positions):
    head_dim = head_vec.shape[-1]
    half_dim = head_dim // 2
    inv_freq = ROPE_BASE ** (-2.0 * jnp.arange(half_dim, dtype=jnp.float32) / head_dim)
    angles = positions.astype(jnp.float32)[:, None] * inv_freq[None, :]
    cos_table = jnp.cos(angles)[:, None, :]
    sin_table = jnp.sin(angles)[:, None, :]
    vec_wide = head_vec.astype(jnp.float32)
    lower_half = vec_wide[..., :half_dim]
    upper_half = vec_wide[..., half_dim:]
    return jnp.concatenate([lower_half * cos_table - upper_half * sin_table, upper_half * cos_table + lower_half * sin_table], axis=-1).astype(jnp.bfloat16)


def write_slot(cache, new_rows, lengths):
    slot_hit = jnp.arange(cache.shape[1])[None, :, None, None] == lengths[:, None, None, None]
    return jnp.where(slot_hit, new_rows[:, None], cache)


def attend(query_rot, k_full, v_full, lengths):
    head_dim = query_rot.shape[-1]
    scores = jnp.einsum('bhd,bshd->bhs', query_rot, k_full, preferred_element_type=jnp.float32) * (head_dim ** -0.5)
    slot_ok = jnp.arange(k_full.shape[1])[None, None, :] <= lengths[:, None, None]
    scores = jnp.where(slot_ok, scores, -1e30)
    attn_probs = jax.nn.softmax(scores, axis=-1).astype(jnp.bfloat16)
    attn_mixed = jnp.einsum('bhs,bshd->bhd', attn_probs, v_full, preferred_element_type=jnp.float32)
    return attn_mixed.astype(jnp.bfloat16).reshape(query_rot.shape[0], -1)


def sharded_norm(h_val, gain, shift, width_all):
    moments = jnp.stack([jnp.sum(h_val, axis=1), jnp.sum(h_val * h_val, axis=1)], axis=1)
    moments = lax.psum(moments, 'x')
    mean_row = moments[:, 0:1] / width_all
    var_row = moments[:, 1:2] / width_all - mean_row * mean_row
    scaled = (h_val - mean_row) * lax.rsqrt(var_row + LN_EPS)
    return (scaled * gain.astype(jnp.float32) + shift.astype(jnp.float32)).astype(jnp.bfloat16)


def solution(mesh):
    x_size = mesh.shape['x']
    cache_spec = P('dp', None, 'y', None)
    width_spec = P('x')
    in_specs = (P('dp', 'x'), P('x', 'y'), P('y'), P('y', 'x'), width_spec, width_spec, width_spec, P('x', None, 'y'), P(None, 'y'), P('y', 'x'), width_spec, width_spec, width_spec, cache_spec, cache_spec, P('dp'), P('dp'))
    out_specs = (P('dp', 'x'), cache_spec, cache_spec)

    def local_step(hidden, w_qkv, b_qkv, w_out, b_out, attn_gain, attn_shift, w_up, b_up, w_down, b_down, mlp_gain, mlp_shift, k_cache, v_cache, positions, lengths):
        row_count, width_local = hidden.shape
        width_all = width_local * x_size
        local_heads, head_dim = k_cache.shape[2], k_cache.shape[3]
        qkv_part = jnp.dot(hidden, w_qkv, preferred_element_type=jnp.float32).astype(jnp.bfloat16)
        qkv_sum = lax.psum(qkv_part, 'x')
        qkv_vals = (qkv_sum.astype(jnp.float32) + b_qkv.astype(jnp.float32)).astype(jnp.bfloat16)
        qkv_vals = qkv_vals.reshape(row_count, local_heads, 3, head_dim)
        query_rot = apply_rotary(qkv_vals[:, :, 0], positions)
        k_full = write_slot(k_cache, apply_rotary(qkv_vals[:, :, 1], positions), lengths)
        v_full = write_slot(v_cache, qkv_vals[:, :, 2], lengths)
        attn_out = attend(query_rot, k_full, v_full, lengths)
        proj_part = jnp.dot(attn_out, w_out, preferred_element_type=jnp.float32).astype(jnp.bfloat16)
        proj_sum = lax.psum(proj_part, 'y')
        h_attn = DEEP_ALPHA * hidden.astype(jnp.float32) + proj_sum.astype(jnp.float32) + b_out.astype(jnp.float32)
        normed = sharded_norm(h_attn, attn_gain, attn_shift, width_all)
        up_part = jnp.einsum('bd,dtf->btf', normed, w_up, preferred_element_type=jnp.float32).astype(jnp.bfloat16)
        up_sum = lax.psum(up_part, 'x').astype(jnp.float32) + b_up.astype(jnp.float32)
        gated_act = (jax.nn.gelu(up_sum[:, 0], approximate=True) * up_sum[:, 1]).astype(jnp.bfloat16)
        down_part = jnp.dot(gated_act, w_down, preferred_element_type=jnp.float32).astype(jnp.bfloat16)
        down_sum = lax.psum(down_part, 'y')
        h_mlp = DEEP_ALPHA * normed.astype(jnp.float32) + down_sum.astype(jnp.float32) + b_down.astype(jnp.float32)
        result = sharded_norm(h_mlp, mlp_gain, mlp_shift, width_all)
        return result, k_full, v_full

    return jax.shard_map(local_step, mesh=mesh, in_specs=in_specs, out_specs=out_specs, check_vma=False)
```

profile of v0, /device:TPU:0, one launch (start us, length us, event | category | flops | bytes accessed | tf_op | source)
XLA Modules:
  0.0 410.2 jit_solution(2417985547040999964)
XLA Ops:
  7.2 0.0 copy-start
  7.2 0.0 all-reduce.5.cloned.1.call-start
  7.2 3.0 convolution_convert_fusion.1
  10.2 0.0 all-reduce.5.cloned.1.call-update
  10.2 0.0 all-reduce.7.cloned.1.call-start
  10.3 0.7 convert_element_type.97
  10.9 0.7 convert_element_type.101
  11.6 0.8 iota_compare_fusion.1
  12.4 0.5 multiply_cosine_fusion
  12.9 69.6 %all-reduce.5.cloned.1.call-done = bf16[1024,768]{1,0:T(8,128)(2,1)} async-done(((bf16[1024,768]{1,0:T(8,128)(2,1)}), bf16[1024,768]{1,0:T(8,128)(2,1)}) %all-reduce.5.cloned.1.call-update) | async-done | bytes 1572880 | tf_op jit(solution)/shard_map/psum | solution.py:61
  82.5 1.7 add_convert_fusion
  84.2 1.6 copy.29
  85.8 1.6 slice_bitcast_fusion.2
  87.4 0.3 subtract_convert_fusion
  87.8 0.1 maximum_convert_fusion
  87.9 31.5 %multiply_reduce_fusion.1 = (f32[1024,4,64]{0,1,2:T(4,128)}, bf16[1024,64,4,64]{0,3,2,1:T(8,128)(2,1)}) fusion(f32[1024,4,64]{0,2,1:T(8,128)S(1)} %get-tuple-element.28, bf16[1024,64,4,64]{0,3,2,1:T(8,128)(2,1)} %param.30, bf16[1024,4,64]{0,2,1:T(8,128)(2,1)S(1)} %get-tuple-element.29, pred[1024,64]{0,1:T(8,128)(4,1)S(1)} %get-tuple-element.27), kind=kLoop, calls=%fused_computation.3 | loop fusion | flops 66846720 | bytes 69795840
  119.4 2.2 fusion.17
  121.7 0.7 copy.47
  122.3 0.0 copy-start.2
  122.4 0.0 copy-start.5
  122.4 0.0 copy-start.6
  122.4 0.0 copy-start.7
  122.4 0.0 copy-start.1
  122.4 23.8 %multiply_reduce_fusion = (bf16[1024,4,64]{0,2,1:T(8,128)(2,1)S(1)}, bf16[1024,64,4,64]{0,3,2,1:T(8,128)(2,1)}) fusion(f32[1024,4,64]{0,1,2:T(4,128)S(1)} %copy.47, bf16[1024,64,4,64]{0,3,2,1:T(8,128)(2,1)} %param.31, bf16[1024,4,64]{0,2,1:T(8,128)(2,1)S(1)} %get-tuple-element.11, pred[1024,64]{0,1:T(8,128)(4,1)S(1)} %get-tuple-element.27), kind=kLoop, calls=%fused_computation.2 | loop fusion | flops 66846720 | bytes 69271552 | tf_op jit(solution)/shard_map/bhs,bshd->bhd/dot_general | solution.py:36
  146.2 0.0 copy-done.2
  146.3 1.1 convolution_convert_fusion.2
  147.4 0.0 all-reduce.7.cloned.1.call-update
  147.4 0.0 all-reduce.9.cloned.1.call-start
  147.5 32.8 %all-reduce.7.cloned.1.call-done = bf16[1024,256]{1,0:T(8,128)(2,1)} async-done(((bf16[1024,256]{1,0:T(8,128)(2,1)}), bf16[1024,256]{1,0:T(8,128)(2,1)}) %all-reduce.7.cloned.1.call-update) | async-done | bytes 524304 | tf_op jit(solution)/shard_map/psum | solution.py:69
  180.4 1.5 fusion.25
  181.8 11.8 %psum.44 = f32[1024,2]{0,1:T(2,128)S(1)} all-reduce(f32[1024,2]{0,1:T(2,128)S(1)} %pad_maximum_fusion.1), channel_id=1, replica_groups=mesh['dp'=2,'x'=4,'y'=4] {'x'}, use_global_device_ids=true, to_apply=%region_6.7 | all-reduce | flops 2048 | bytes 16384 | tf_op jit(solution)/shard_map/psum | solution.py:42
  193.7 1.4 add_convert_fusion.2
  195.1 0.0 copy-start.3
  195.1 3.3 convolution_convert_fusion
  198.4 0.0 all-reduce.9.cloned.1.call-update
  198.4 0.2 all-reduce.11.cloned.1.call-start
  198.7 0.0 copy-start.4
  198.7 151.0 %all-reduce.9.cloned.1.call-done = bf16[1024,2,1024]{2,0,1:T(8,128)(2,1)} async-done(((bf16[1024,2,1024]{2,0,1:T(8,128)(2,1)}), bf16[1024,2,1024]{2,0,1:T(8,128)(2,1)}) %all-reduce.9.cloned.1.call-update) | async-done | bytes 4194320 | tf_op jit(solution)/shard_map/psum | solution.py:73
  349.7 3.4 convert_add_fusion
  353.1 0.0 copy-start.8
  353.1 0.0 copy-start.9
  353.1 0.0 copy-start.10
  353.1 2.5 fusion.18
  355.6 0.0 all-reduce.11.cloned.1.call-update
  355.7 32.4 %all-reduce.11.cloned.1.call-done = bf16[1024,256]{1,0:T(8,128)(2,1)} async-done(((bf16[1024,256]{1,0:T(8,128)(2,1)}), bf16[1024,256]{1,0:T(8,128)(2,1)}) %all-reduce.11.cloned.1.call-update) | async-done | bytes 524304 | tf_op jit(solution)/shard_map/psum | solution.py:76
  388.1 1.5 fusion.26
  389.6 11.8 %psum.47 = f32[1024,2]{0,1:T(2,128)S(1)} all-reduce(f32[1024,2]{0,1:T(2,128)S(1)} %pad_maximum_fusion.2), channel_id=1, replica_groups=mesh['dp'=2,'x'=4,'y'=4] {'x'}, use_global_device_ids=true, to_apply=%region_11.12 | all-reduce | flops 2048 | bytes 16384 | tf_op jit(solution)/shard_map/psum | solution.py:42
  401.4 2.2 add_convert_fusion.1
  (22 shorter events, 0.1 us)
Async XLA Ops:
  7.2 188.0 %copy-start = (bf16[256,2,1024]{2,1,0:T(2,128)(2,1)S(1)}, bf16[256,2,1024]{2,1,0:T(2,128)(2,1)}, u32[]{:S(2)}) copy-start(bf16[256,2,1024]{2,1,0:T(2,128)(2,1)} %param.24) | copy-start | bytes 3145732
  7.2 75.3 %all-reduce.5.cloned.1.call-start = ((), (), s32[]{:S(2)}) async-start(), calls=%async_computation | async-start | bytes 3145728 | tf_op jit(solution)/shard_map/psum | solution.py:61
  10.2 170.2 %all-reduce.7.cloned.1.call-start = ((), (), s32[]{:S(2)}) async-start(), calls=%async_computation.1 | async-start | bytes 1048576 | tf_op jit(solution)/shard_map/psum | solution.py:69
  122.3 23.9 %copy-start.2 = (bf16[256,256]{1,0:T(8,128)(2,1)S(1)}, bf16[256,256]{1,0:T(8,128)(2,1)}, u32[]{:S(2)}) copy-start(bf16[256,256]{1,0:T(8,128)(2,1)} %param.20) | copy-start | bytes 393220
  122.4 25.1 %copy-start.5 = (bf16[256]{0:T(256)(128)(2,1)S(1)}, bf16[256]{0:T(256)(128)(2,1)}, u32[]{:S(2)}) copy-start(bf16[256]{0:T(256)(128)(2,1)} %param.21) | copy-start | bytes 1540
  122.4 25.1 %copy-start.6 = (bf16[256]{0:T(256)(128)(2,1)S(1)}, bf16[256]{0:T(256)(128)(2,1)}, u32[]{:S(2)}) copy-start(bf16[256]{0:T(256)(128)(2,1)} %param.22) | copy-start | bytes 1540
  122.4 25.1 %copy-start.7 = (bf16[256]{0:T(256)(128)(2,1)S(1)}, bf16[256]{0:T(256)(128)(2,1)}, u32[]{:S(2)}) copy-start(bf16[256]{0:T(256)(128)(2,1)} %param.23) | copy-start | bytes 1540
  122.4 58.0 %copy-start.1 = (bf16[1024,256]{1,0:T(8,128)(2,1)S(1)}, bf16[1024,256]{1,0:T(8,128)(2,1)}, u32[]{:S(2)}) copy-start(bf16[1024,256]{1,0:T(8,128)(2,1)} %param.17) | copy-start | bytes 1572868
  147.4 202.3 %all-reduce.9.cloned.1.call-start = ((), (), s32[]{:S(2)}) async-start(), calls=%async_computation.2 | async-start | bytes 8388608 | tf_op jit(solution)/shard_map/psum | solution.py:73
  195.1 3.5 copy-start.3
  198.4 189.6 %all-reduce.11.cloned.1.call-start = ((), (), s32[]{:S(2)}) async-start(), calls=%async_computation.3 | async-start | bytes 1048576 | tf_op jit(solution)/shard_map/psum | solution.py:76
  198.7 154.4 %copy-start.4 = (bf16[1024,256]{1,0:T(8,128)(2,1)S(1)}, bf16[1024,256]{1,0:T(8,128)(2,1)}, u32[]{:S(2)}) copy-start(bf16[1024,256]{1,0:T(8,128)(2,1)} %param.26) | copy-start | bytes 1572868
  353.1 2.5 copy-start.8
  353.1 2.5 copy-start.9
  353.1 2.6 copy-start.10
Sparse Core Ops, SparseCore 0:
  10.9 71.5 all-reduce.4
  147.5 32.7 all-reduce.6
  198.6 151.0 all-reduce.8
  355.7 32.2 all-reduce.10
where the time goes:
time: 411 us; the launch traced here: 410 us
  waiting for transfers between devices  286 us (70%)
  other arithmetic  74 us (18%)
  blocking collectives  23.7 us (6%)
  between operations  14.1 us (3%)
  matrix products  9.85 us (2%)
    psum x1, waiting for transfers between devices, local_step(): lax.psum(up_part, 'x').astype(jnp.float32) + b_up.astype(jnp.float32)  151 us
    psum x1, waiting for transfers between devices, local_step(): qkv_sum = lax.psum(qkv_part, 'x')  69.6 us
    psum x1, waiting for transfers between devices, local_step(): proj_sum = lax.psum(proj_part, 'y')  32.8 us
    psum x1, waiting for transfers between devices, local_step(): down_sum = lax.psum(down_part, 'y')  32.4 us
    unnamed x2, other arithmetic  31.6 us
    dot_general x1, other arithmetic, attend(): jnp.einsum('bhs,bshd->bhd', attn_probs, v_full, preferred_element_type=jn...  23.8 us
    psum x2, blocking collectives, sharded_norm(): moments = lax.psum(moments, 'x')  23.7 us
  transfers between devices with their start and end apart: 4, of which 4 were waited for; matrix products, arithmetic and copies ran while one was open for 1% of the time, Pallas kernels for 0%

commit v1 on v0

v1 whole, which is shorter than its diff:
```python
import functools
import math
import jax
import jax.numpy as jnp
from jax import lax
from jax.experimental import pallas as pl
from jax.experimental.pallas import tpu as pltpu
from jax.sharding import PartitionSpec as P

DEEP_ALPHA = math.sqrt(140.0)
LN_EPS = 1e-5
ROPE_BASE = 10000.0
MESH = pl.DeviceIdType.MESH
VMEM = pltpu.VMEM
F32 = jnp.float32
BF16 = jnp.bfloat16


def where_am_i():
    dp, x, y = lax.axis_index("dp"), lax.axis_index("x"), lax.axis_index("y")
    core, chip = lax.rem(y, 2), y // 2
    return dp, x, y, core, chip, core * 2 + chip


def remote(src, dst, send, recv, device):
    return pltpu.make_async_remote_copy(
        src_ref=src, dst_ref=dst, send_sem=send, recv_sem=recv, device_id=device, device_id_type=MESH)


def greet(devices):
    barrier = pltpu.get_barrier_semaphore()
    for device in devices:
        pl.semaphore_signal(barrier, inc=1, device_id=device, device_id_type=MESH)
    pl.semaphore_wait(barrier, len(devices))


def qkv_kernel(hid_ref, w_ref, b_ref, vec_ref, cos_ref, sin_ref,
               q_ref, k_ref, v_ref, hres_ref, vecs_ref,
               hbuf, wbuf, vbuf, hz_s, hz_r, hy_s, hy_r, hd_s, hd_r, wz_s, wz_r, wx_s, wx_r, vz_s, vz_r):
    dp, x, y, core, chip, piece = where_am_i()
    mate = (dp, x, chip * 2 + 1 - core)
    across = (dp, x, (1 - chip) * 2 + core)
    twin = (1 - dp, x, y)
    peers = [(dp, lax.rem(x + j, 4), y) for j in (1, 2, 3)]
    source = [lax.rem(x + 4 - j, 4) for j in (0, 1, 2, 3)]
    greet(peers + [mate, across, twin])

    row0 = pl.multiple_of(piece * 256, 256)
    hz, wz, vz = [], [], []
    for j in (1, 2, 3):
        c = remote(hid_ref.at[pl.ds(row0, 256)], hbuf.at[piece, x], hz_s.at[j], hz_r.at[j], peers[j - 1])
        c.start()
        hz.append(c)
    half0 = pl.multiple_of(dp * 128, 128)
    for j in (1, 2, 3):
        c = remote(w_ref.at[pl.ds(half0, 128)], wbuf.at[x, dp], wz_s.at[j], wz_r.at[j], peers[j - 1])
        c.start()
        wz.append(c)
        c = remote(vec_ref, vbuf.at[x], vz_s.at[j], vz_r.at[j], peers[j - 1])
        c.start()
        vz.append(c)
    for part in range(4):
        hbuf[part, x] = hid_ref[part * 256:(part + 1) * 256, :]
    for half in range(2):
        wbuf[x, half] = w_ref[half * 128:(half + 1) * 128, :]
    vbuf[x] = vec_ref[...]

    hy, hd, wx = [], [], []
    for j in (1, 2, 3):
        hz[j - 1].wait_recv()
        c = remote(hbuf.at[piece, source[j]], hbuf.at[piece, source[j]], hy_s.at[j], hy_r.at[j], across)
        c.start()
        hy.append(c)
    for j in (1, 2, 3):
        hy[j - 1].wait_recv()
        both = hbuf.at[pl.ds(core * 2, 2), source[j]]
        c = remote(both, both, hd_s.at[j], hd_r.at[j], mate)
        c.start()
        hd.append(c)
    for j in (1, 2, 3):
        wz[j - 1].wait_recv()
        block = wbuf.at[source[j], dp]
        c = remote(block, block, wx_s.at[j], wx_r.at[j], twin)
        c.start()
        wx.append(c)
    for c in hd + vz + wx:
        c.wait_recv()

    for s in range(4):
        hres_ref[:, s * 256:(s + 1) * 256] = hbuf[x, s, pl.ds(pl.multiple_of(piece * 64, 64), 64), :]
        vecs_ref[:, s * 256:(s + 1) * 256] = vbuf[s]

    def rows(part, _):
        acc = jnp.dot(hbuf[part, 0], wbuf[0].reshape(256, 768), preferred_element_type=F32)
        for s in (1, 2, 3):
            acc += jnp.dot(hbuf[part, s], wbuf[s].reshape(256, 768), preferred_element_type=F32)
        acc = (acc + b_ref[...].astype(F32)).astype(BF16).astype(F32)
        lanes = pl.ds(pl.multiple_of(part * 256, 256), 256)
        cos, sin = cos_ref[:, lanes], sin_ref[:, lanes]
        acc = acc.T
        for head in range(4):
            base = head * 192
            for off, ref in ((0, q_ref), (64, k_ref)):
                low, high = acc[base + off:base + off + 32], acc[base + off + 32:base + off + 64]
                ref[head * 64:head * 64 + 32, lanes] = (low * cos - high * sin).astype(BF16)
                ref[head * 64 + 32:head * 64 + 64, lanes] = (high * cos + low * sin).astype(BF16)
            v_ref[head * 64:(head + 1) * 64, lanes] = acc[base + 128:base + 192].astype(BF16)
        return 0

    lax.fori_loop(0, 4, rows, 0)
    for c in hz + wz + vz + hy + hd + wx:
        c.wait_send()


def cache_kernel(len_ref, q_ref, kn_ref, vn_ref, k_ref, v_ref, ko_ref, vo_ref, attn_ref, sc_ref):
    slots = k_ref.shape[0]
    lens = len_ref[...]
    k_new, v_new = kn_ref[...], vn_ref[...]
    mine = pl.program_id(0) == lax.axis_index("x")

    def hit(s):
        return jnp.broadcast_to((lens - s).astype(F32), k_new.shape).astype(BF16) == 0

    @pl.when(jnp.logical_not(mine))
    def _():
        def body(s, _):
            m = hit(s)
            ko_ref[s, 0] = jnp.where(m, k_new, k_ref[s, 0])
            vo_ref[s, 0] = jnp.where(m, v_new, v_ref[s, 0])
            return 0
        lax.fori_loop(0, slots, body, 0, unroll=4)
        attn_ref[...] = jnp.zeros_like(attn_ref)

    @pl.when(mine)
    def _():
        q = q_ref[...].astype(F32)

        def keys(s, _):
            kk = jnp.where(hit(s), k_new, k_ref[s, 0])
            ko_ref[s, 0] = kk
            sc_ref[pl.ds(s, 1), :] = jnp.sum(kk.astype(F32) * q, axis=0, keepdims=True)
            return 0
        lax.fori_loop(0, slots, keys, 0, unroll=4)
        sc = sc_ref[...] * (64 ** -0.5)
        sc = jnp.where(lax.broadcasted_iota(jnp.int32, sc.shape, 0) <= lens, sc, -1e30)
        e = jnp.exp(sc - jnp.max(sc, axis=0, keepdims=True))
        sc_ref[...] = (e / jnp.sum(e, axis=0, keepdims=True)).astype(BF16).astype(F32)

        def values(s, acc):
            vv = jnp.where(hit(s), v_new, v_ref[s, 0])
            vo_ref[s, 0] = vv
            return acc + vv.astype(F32) * sc_ref[pl.ds(s, 1), :]
        acc = lax.fori_loop(0, slots, values, jnp.zeros(k_new.shape, F32), unroll=4)
        attn_ref[...] = acc.astype(BF16)


def whole_row_norm(h, gain, shift):
    mean = jnp.mean(h, axis=-1, keepdims=True)
    dev = h - mean
    var = jnp.mean(dev * dev, axis=-1, keepdims=True)
    return (dev * lax.rsqrt(var + LN_EPS) * gain + shift).astype(BF16)


def mlp_kernel(attn_ref, w0_ref, w1_ref, w2_ref, w3_ref, hres_ref, vecs_ref, bup_ref,
               out_ref,
               wg, wv, wd, wo, p1, s1d, r1d, s1y, r1y, zfull,
               keep, sd, rd, sy, ry, sz, rz, ob, ofull,
               a_s, a_r, zz_s, zz_r, zy_s, zy_r, zd_s, zd_r,
               md_s, md_r, my_s, my_r, mz_s, mz_r, oz_s, oz_r, oy_s, oy_r, od_s, od_r):
    dp, x, y, core, chip, piece = where_am_i()
    mate = (dp, x, chip * 2 + 1 - core)
    across = (dp, x, (1 - chip) * 2 + core)
    peers = [(dp, lax.rem(x + j, 4), y) for j in (1, 2, 3)]
    source = [lax.rem(x + 4 - j, 4) for j in (0, 1, 2, 3)]
    sends = []

    def go(src, dst, send, recv, device):
        c = remote(src, dst, send, recv, device)
        c.start()
        sends.append(c)
        return c

    greet(peers + [mate, across])
    for j, ref in enumerate((w0_ref, w1_ref, w2_ref, w3_ref)):
        at = pl.ds(pl.multiple_of(source[j] * 256, 256), 256)
        wg[at, :] = ref[0:256, :]
        wv[at, :] = ref[256:512, :]
        wd[:, at] = ref[512:768, :]
        wo[:, at] = ref[768:1024, :]

    mine = attn_ref[:, pl.ds(pl.multiple_of(x * 256, 256), 256)].astype(F32).T.astype(BF16)
    p1[...] = jnp.dot(mine, wo[...], preferred_element_type=F32)
    s1d[...] = p1[pl.ds(pl.multiple_of((1 - core) * 128, 128), 128), :].astype(BF16)
    c = go(s1d, r1d, a_s.at[0], a_r.at[0], mate)
    c.wait_recv()
    give = (1 - chip) * 64
    hold = chip * 64
    base = core * 128
    s1y[...] = (p1[pl.ds(pl.multiple_of(base + give, 64), 64), :]
                + r1d[pl.ds(pl.multiple_of(give, 64), 64), :].astype(F32)).astype(BF16)
    c = go(s1y, r1y, a_s.at[1], a_r.at[1], across)
    h = (p1[pl.ds(pl.multiple_of(base + hold, 64), 64), :]
         + r1d[pl.ds(pl.multiple_of(hold, 64), 64), :].astype(F32))
    c.wait_recv()
    h = h + r1y[...].astype(F32)
    h = DEEP_ALPHA * hres_ref[...].astype(F32) + (h + vecs_ref[0:1, :])
    zfull[x, piece] = whole_row_norm(h, vecs_ref[1:2, :], vecs_ref[2:3, :])

    own = zfull.at[x, piece]
    zz = [go(own, own, zz_s.at[j], zz_r.at[j], peers[j - 1]) for j in (1, 2, 3)]
    zy = [go(own, own, zy_s.at[0], zy_r.at[0], across)]
    for j in (1, 2, 3):
        zz[j - 1].wait_recv()
        block = zfull.at[source[j], piece]
        zy.append(go(block, block, zy_s.at[j], zy_r.at[j], across))
        if j == 1:
            zy[0].wait_recv()
            both = zfull.at[x, pl.ds(core * 2, 2)]
            zd = [go(both, both, zd_s.at[0], zd_r.at[0], mate)]

    def mlp(j):
        z = zfull[source[j]].reshape(256, 1024)
        gate = jnp.dot(z, wg[...], preferred_element_type=F32) + bup_ref[0:1, :]
        value = jnp.dot(z, wv[...], preferred_element_type=F32) + bup_ref[1:2, :]
        g = (jax.nn.gelu(gate, approximate=True) * value).astype(BF16)
        p1[...] = jnp.dot(g, wd[...], preferred_element_type=F32)
        sd[j] = p1[pl.ds(pl.multiple_of((1 - core) * 128, 128), 128), :].astype(BF16)
        keep[j] = p1[pl.ds(pl.multiple_of(base, 128), 128), :]
        return go(sd.at[j], rd.at[j], md_s.at[j], md_r.at[j], mate)

    def pair_sum(j, c):
        c.wait_recv()
        at = pl.ds(pl.multiple_of(give, 64), 64)
        sy[j] = (keep[j, at, :] + rd[j, at, :].astype(F32)).astype(BF16)
        return go(sy.at[j], ry.at[j], my_s.at[j], my_r.at[j], across)

    def chip_sum(j, c):
        c.wait_recv()
        at = pl.ds(pl.multiple_of(hold, 64), 64)
        total = keep[j, at, :] + rd[j, at, :].astype(F32) + ry[j].astype(F32)
        if j == 0:
            keep[0, 0:64, :] = total
            return None
        sz[j] = total.astype(BF16)
        back = (dp, source[j], y)
        return go(sz.at[j], rz.at[j], mz_s.at[j], mz_r.at[j], back)

    md, my, mz = {}, {}, {}
    for t in range(6):
        if t < 4:
            if t > 0:
                zy[t].wait_recv()
                both = zfull.at[source[t], pl.ds(core * 2, 2)]
                zd.append(go(both, both, zd_s.at[t], zd_r.at[t], mate))
            zd[t].wait_recv()
            md[t] = mlp(t)
        if 1 <= t < 5:
            my[t - 1] = pair_sum(t - 1, md[t - 1])
        if 2 <= t:
            mz[t - 2] = chip_sum(t - 2, my[t - 2])
    h = keep[0, 0:64, :]
    for j in (1, 2, 3):
        mz[j].wait_recv()
        h = h + rz[j].astype(F32)
    h = DEEP_ALPHA * zfull[x, piece].astype(F32) + h + vecs_ref[3:4, :]
    o = whole_row_norm(h, vecs_ref[4:5, :], vecs_ref[5:6, :])

    for s in range(4):
        ob[s] = o[:, s * 256:(s + 1) * 256]
    ofull[x, piece] = ob[x]
    oz = [go(ob.at[lax.rem(x + j, 4)], ofull.at[x, piece], oz_s.at[j], oz_r.at[j], peers[j - 1]) for j in (1, 2, 3)]
    oy = []
    for j in range(4):
        if j > 0:
            oz[j - 1].wait_recv()
        block = ofull.at[source[j], piece]
        oy.append(go(block, block, oy_s.at[j], oy_r.at[j], across))
    od = []
    for j in range(4):
        oy[j].wait_recv()
        both = ofull.at[source[j], pl.ds(core * 2, 2)]
        od.append(go(both, both, od_s.at[j], od_r.at[j], mate))
    for c in od:
        c.wait_recv()
    out_ref[...] = ofull[...].reshape(1024, 256)
    for c in sends:
        c.wait_send()


def solution(mesh):
    cache_spec = P('dp', None, 'y', None)
    width_spec = P('x')
    in_specs = (P('dp', 'x'), P('x', 'y'), P('y'), P('y', 'x'), width_spec, width_spec, width_spec, P('x', None, 'y'), P(None, 'y'), P('y', 'x'), width_spec, width_spec, width_spec, cache_spec, cache_spec, P('dp'), P('dp'))
    out_specs = (P('dp', 'x'), cache_spec, cache_spec)
    vmem = pl.BlockSpec(memory_space=VMEM)
    dma = pltpu.SemaphoreType.DMA

    def local_step(hidden, w_qkv, b_qkv, w_out, b_out, attn_gain, attn_shift, w_up, b_up, w_down, b_down, mlp_gain, mlp_shift, k_cache, v_cache, positions, lengths):
        x = lax.axis_index('x')
        inv_freq = ROPE_BASE ** (-2.0 * jnp.arange(32, dtype=F32) / 64)
        angles = inv_freq[:, None] * positions.astype(F32)[None, :]
        cos, sin = jnp.cos(angles), jnp.sin(angles)
        vec = jnp.stack([v.astype(F32) for v in (b_out, attn_gain, attn_shift, b_down, mlp_gain, mlp_shift, b_out, b_out)])
        row = jax.ShapeDtypeStruct((256, 1024), BF16)
        q, k_new, v_new, hres, vecs = pl.pallas_call(
            qkv_kernel,
            name="gather_qkv",
            out_shape=(row, row, row, jax.ShapeDtypeStruct((64, 1024), BF16), jax.ShapeDtypeStruct((8, 1024), F32)),
            in_specs=[vmem] * 6,
            out_specs=(vmem,) * 5,
            scratch_shapes=[
                VMEM((4, 4, 256, 256), BF16),
                VMEM((4, 2, 128, 768), BF16),
                VMEM((4, 8, 256), F32),
            ] + [dma((4,))] * 12,
            compiler_params=pltpu.CompilerParams(collective_id=0, has_side_effects=True),
            cost_estimate=pl.CostEstimate(flops=2 * 1024 * 1024 * 768, bytes_accessed=8 << 20, transcendentals=0),
        )(hidden, w_qkv, b_qkv.reshape(1, 768), vec, cos, sin)

        packs = []
        for j in range(4):
            t = lax.rem(x + j, 4) * 256
            up = lax.dynamic_slice_in_dim(w_up, t, 256, axis=2)
            down = lax.dynamic_slice_in_dim(w_down, t, 256, axis=0)
            packs.append(jnp.concatenate([up[:, 0], up[:, 1], down, w_out], axis=0))
        q, *packs = lax.optimization_barrier((q, *packs))
        moved = [packs[0]] + [lax.ppermute(packs[j], 'x', [(i, (i + j) % 4) for i in range(4)]) for j in (1, 2, 3)]
        bup = lax.dynamic_slice_in_dim(b_up, x * 256, 256, axis=1).astype(F32)

        k_t, v_t = k_cache.transpose(1, 2, 3, 0), v_cache.transpose(1, 2, 3, 0)
        big = pl.BlockSpec((64, 1, 64, 256), lambda r, h: (0, h, 0, r))
        small = pl.BlockSpec((64, 256), lambda r, h: (h, r))
        k_full, v_full, attn = pl.pallas_call(
            cache_kernel,
            name="cache_attend",
            grid=(4, 4),
            out_shape=(jax.ShapeDtypeStruct(k_t.shape, BF16), jax.ShapeDtypeStruct(v_t.shape, BF16), row),
            in_specs=[pl.BlockSpec((1, 256), lambda r, h: (0, r)), small, small, small, big, big],
            out_specs=(big, big, small),
            scratch_shapes=[VMEM((64, 256), F32)],
            cost_estimate=pl.CostEstimate(flops=4 * 10 ** 9, bytes_accessed=128 << 20, transcendentals=0),
        )(lengths.reshape(1, 1024), q, k_new, v_new, k_t, v_t)

        out = pl.pallas_call(
            mlp_kernel,
            name="project_mlp",
            out_shape=jax.ShapeDtypeStruct((1024, 256), BF16),
            in_specs=[vmem] * 8,
            out_specs=vmem,
            scratch_shapes=[
                VMEM((1024, 256), BF16), VMEM((1024, 256), BF16), VMEM((256, 1024), BF16), VMEM((256, 1024), BF16),
                VMEM((256, 1024), F32),
                VMEM((128, 1024), BF16), VMEM((128, 1024), BF16), VMEM((64, 1024), BF16), VMEM((64, 1024), BF16),
                VMEM((4, 4, 64, 1024), BF16),
                VMEM((4, 128, 1024), F32),
                VMEM((4, 128, 1024), BF16), VMEM((4, 128, 1024), BF16),
                VMEM((4, 64, 1024), BF16), VMEM((4, 64, 1024), BF16),
                VMEM((4, 64, 1024), BF16), VMEM((4, 64, 1024), BF16),
                VMEM((4, 64, 256), BF16),
                VMEM((4, 4, 64, 256), BF16),
            ] + [dma((4,))] * 20,
            compiler_params=pltpu.CompilerParams(collective_id=1, has_side_effects=True),
            cost_estimate=pl.CostEstimate(flops=4 * 10 ** 9, bytes_accessed=8 << 20, transcendentals=0),
        )(attn, *moved, hres, vecs, bup)
        return out, k_full.transpose(3, 0, 1, 2), v_full.transpose(3, 0, 1, 2)

    return jax.shard_map(local_step, mesh=mesh, in_specs=in_specs, out_specs=out_specs, check_vma=False)
```

time: 411 us -> 182 us (0.44)
  waiting for transfers between devices: 286 us -> 0.01 us
  Pallas kernels: 0 us -> 153 us
  other arithmetic: 74 us -> 5.63 us
  blocking collectives: 23.7 us -> 0 us
  between operations: 14.1 us -> 0.76 us
  local copies, waits for them, and re-layouts: 2.38 us -> 13.6 us
  matrix products: 9.85 us -> 0 us
  starting transfers between devices: 0.34 us -> 8.95 us
    psum x4 -> x0, waiting for transfers between devices: 286 us -> none  [the longest x1 151 us: local_step(): lax.psum(up_part, 'x').astype(jnp.float32) + b_up.astype(jnp.float32)]
    pallas_call x0 -> x3, Pallas kernels: none -> 153 us  [the longest x1 57.3 us: local_step(): pl.pallas_call(mlp_kernel, name='project_mlp', out_shape=jax.ShapeDtypeSt...]
    unnamed x2 -> x0, other arithmetic: 31.6 us -> none
    dot_general x1 -> x0, other arithmetic: 23.8 us -> none  [attend(): jnp.einsum('bhs,bshd->bhd', attn_probs, v_full, preferred_element_type=jn...]
    psum x2 -> x0, blocking collectives: 23.7 us -> none  [sharded_norm(): moments = lax.psum(moments, 'x')]
    dot_general x4 -> x0, matrix products: 9.85 us -> none  [the longest x1 3.27 us: local_step(): jnp.einsum('bd,dtf->btf', normed, w_up, preferred_element_type=jnp.float32)]
    ppermute x0 -> x3, starting transfers between devices: none -> 8.95 us  [local_step(): lax.ppermute(packs[j], 'x', [(i, (i + j) % 4) for i in range(4)])]
    convert_element_type x12 -> x2, other arithmetic: 6.68 us -> 1.95 us  [the longest x1 1.25 us: local_step(): bup = lax.dynamic_slice_in_dim(b_up, x * 256, 256, axis=1).astype(F32)]
  transfers between devices with their start and end apart: 4 -> 3, of which waited for: 4 -> 0; matrix products, arithmetic and copies ran while one was open for 1% -> 1% of each run, Pallas kernels for 0% -> 27%
where the time goes in v1:
time: 182 us
  Pallas kernels  153 us (84%)
  local copies, waits for them, and re-layouts  13.6 us (7%)
  starting transfers between devices  8.95 us (5%)
  other arithmetic  5.63 us (3%)
    pallas_call x1, Pallas kernels, local_step(): pl.pallas_call(mlp_kernel, name='project_mlp', out_shape=jax.ShapeDtypeSt...  57.3 us
    pallas_call x1, Pallas kernels, local_step(): pl.pallas_call(cache_kernel, name='cache_attend', grid=(4, 4), out_shape=...  49.8 us
    pallas_call x1, Pallas kernels, local_step(): pl.pallas_call(qkv_kernel, name='gather_qkv', out_shape=(row, row, row, j...  45.7 us
    ppermute x3, starting transfers between devices, local_step(): lax.ppermute(packs[j], 'x', [(i, (i + j) % 4) for i in range(4)])  8.95 us
    slice x1, local copies, waits for them, and re-layouts, local_step(): packs.append(jnp.concatenate([up[:, 0], up[:, 1], down, w_out], axis=0))  4.06 us
    another operation x7, local copies, waits for them, and re-layouts, local_step(): jnp.stack([v.astype(F32) for v in (b_out, attn_gain, attn_shift, b_down,...  3.98 us
  transfers between devices with their start and end apart: 3, of which 0 were waited for; matrix products, arithmetic and copies ran while one was open for 1% of the time, Pallas kernels for 27%

profile of v1, /device:TPU:0, one launch (start us, length us, event | category | flops | bytes accessed | tf_op | source)
XLA Modules:
  0.0 181.8 jit_solution(7306483778909929203)
XLA Ops:
  0.7 0.7 convert_element_type.4
  1.4 0.7 stack.31
  2.0 0.7 stack.32
  2.7 0.7 stack.33
  3.3 0.7 stack.34
  4.0 0.7 stack.35
  4.7 0.7 stack.36
  5.3 0.6 stack.38.vec_ref
  5.9 1.3 reshape.19.b_ref
  7.2 1.1 constant_dynamic-slice_fusion.5
  8.3 4.1 %constant_dynamic-slice_fusion.1 = (bf16[256,1,256]{2,1,0:T(2,128)(2,1)S(1)}, bf16[256,1,256]{2,1,0:T(2,128)(2,1)S(1)}, bf16[256,1,256]{2,1,0:T(2,128)(2,1)S(1)}...) fusion(bf16[256,2,1024]{2,1,0:T(2,128)(2,1)} %param.24, ...), kind=kLoop, calls=%fused_computation.15 | loop fusion | bytes 2097172 | tf_op jit(solution)/shard_map/slice | solution.py:325
  12.6 1.2 multiply_sine_fusion
  13.8 45.7 %gather_qkv.1 = (bf16[256,1024]{1,0:T(8,128)(2,1)}, bf16[256,1024]{1,0:T(8,128)(2,1)}, bf16[256,1024]{1,0:T(8,128)(2,1)}, bf16[64,1024]{1,0:T(8,128)(2,1)}, f32[8,1024]{1,0:T(8,128)}) custom-call(bf16[1024,256]{1,0:T(8,128)(2,1)} %hid_ref.1, bf16[256,768]{1,0:T(8,128)(2,1)} %w_ref.1, bf16[1,768]{1,0:T(2,128)(2,1)} %reshape.19.b_ref, ...), custom_call_target="tpu_custom_call" | custom-call | flops 1610612736 | bytes 8388608 | tf_op jit(solution)/shard_map/gather_qkv/pallas_call | solution.py:305
  59.5 1.8 %pad_maximum_fusion = (bf16[1024,256]{1,0:T(8,128)(2,1)S(1)}, bf16[1024,256]{1,0:T(8,128)(2,1)S(1)}, bf16[1024,256]{1,0:T(8,128)(2,1)S(1)}, bf16[1024,256]{1,0:T(8,128)(2,1)}) fusion(bf16[256,256]{1,0:T(8,128)(2,1)} %param.20, bf16[256,256]{1,0:T(8,128)(2,1)S(1)} %get-tuple-element.37, bf16[256,256]{1,0:T(8,128)(2,1)S(1)} %get-tuple-element.47, ...), kind=kLoop, calls=%fused_computation | loop fusion | flops 7602176 | bytes 3801088 | tf_op jit(solution)/shard_map/concatenate | solution.py:325
  61.4 4.5 %collective-permute-start = (bf16[1024,256]{1,0:T(8,128)(2,1)S(1)}, bf16[1024,256]{1,0:T(8,128)(2,1)S(1)}, u32[]{:S(2)}, u32[]{:S(2)}) collective-permute-start(bf16[1024,256]{1,0:T(8,128)(2,1)S(1)} %get-tuple-element.22), channel_id=1, source_target_pairs={{0,4},{4,8},{8,12},{12,0},{1,5},{5,9},{9,13},{13,1},{2,6},{6,10},{... | collective-permute-start | bytes 1572872 | tf_op jit(solution)/shard_map/ppermute | solution.py:327
  65.9 3.2 %collective-permute-start.1 = (bf16[1024,256]{1,0:T(8,128)(2,1)S(1)}, bf16[1024,256]{1,0:T(8,128)(2,1)S(1)}, u32[]{:S(2)}, u32[]{:S(2)}) collective-permute-start(bf16[1024,256]{1,0:T(8,128)(2,1)S(1)} %get-tuple-element.23), channel_id=1, source_target_pairs={{0,8},{4,12},{8,0},{12,4},{1,9},{5,13},{9,1},{13,5},{2,10},{6,14},... | collective-permute-start | bytes 1572872 | tf_op jit(solution)/shard_map/ppermute | solution.py:327
  69.0 1.3 collective-permute-start.2
  70.3 1.3 fusion.bup_ref
  71.6 49.8 %cache_attend.1 = (bf16[64,4,64,1024]{3,2,1,0:T(8,128)(2,1)}, bf16[64,4,64,1024]{3,2,1,0:T(8,128)(2,1)}, bf16[256,1024]{1,0:T(8,128)(2,1)}) custom-call(s32[1,1024]{1,0:T(1,128)} %bitcast.23, bf16[256,1024]{1,0:T(8,128)(2,1)} %get-tuple-element.17.q_ref, bf16[256,1024]{1,0:T(8,128)(2,1)} %get-tuple-element.18.kn_ref, ...), custom_call_target="tpu_custom_call" | custom-call | flops 4000000000 | bytes 134217728 | tf_op jit(solution)/shard_map/cache_attend/pallas_call | solution.py:333
  121.4 0.0 collective-permute-done.w1_ref
  121.4 0.0 copy-start
  121.4 0.0 collective-permute-done.1.w2_ref
  121.4 0.0 copy-start.1
  121.4 0.0 collective-permute-done.2.w3_ref
  121.4 0.0 copy-start.2
  121.5 0.7 copy-done
  122.2 0.2 copy-done.1
  122.4 0.2 copy-done.2
  122.6 57.3 %project_mlp.1 = bf16[1024,256]{1,0:T(8,128)(2,1)} custom-call(bf16[256,1024]{1,0:T(8,128)(2,1)} %get-tuple-element.20.attn_ref, bf16[1024,256]{1,0:T(8,128)(2,1)} %get-tuple-element.21.w0_ref, bf16[1024,256]{1,0:T(8,128)(2,1)} %copy-done, bf16[1024,256]{1,0:T(8,128)(2,1)} %copy-done.1, bf16[1024,256]{1,0:T(8,128)(2,1)} %copy-done.2, ...), custom_call_target="tpu_custom_call" | custom-call | flops 4000000000 | bytes 8388608 | tf_op jit(solution)/shard_map/project_mlp/pallas_call | solution.py:344
  179.9 1.9 %copy.45 = bf16[1024,256]{1,0:T(8,128)(2,1)} copy(bf16[1024,256]{1,0:T(8,128)(2,1)} %project_mlp.1) | data formatting | bytes 1048576
  (6 shorter events, 0.2 us)
Async XLA Ops:
  61.4 60.0 %collective-permute-start = (bf16[1024,256]{1,0:T(8,128)(2,1)S(1)}, bf16[1024,256]{1,0:T(8,128)(2,1)S(1)}, u32[]{:S(2)}, u32[]{:S(2)}) collective-permute-start(bf16[1024,256]{1,0:T(8,128)(2,1)S(1)} %get-tuple-element.22), channel_id=1, source_target_pairs={{0,4},{4,8},{8,12},{12,0},{1,5},{5,9},{9,13},{13,1},{2,6},{6,10},{... | collective-permute-start | bytes 1572872 | tf_op jit(solution)/shard_map/ppermute | solution.py:327
  65.9 55.6 %collective-permute-start.1 = (bf16[1024,256]{1,0:T(8,128)(2,1)S(1)}, bf16[1024,256]{1,0:T(8,128)(2,1)S(1)}, u32[]{:S(2)}, u32[]{:S(2)}) collective-permute-start(bf16[1024,256]{1,0:T(8,128)(2,1)S(1)} %get-tuple-element.23), channel_id=1, source_target_pairs={{0,8},{4,12},{8,0},{12,4},{1,9},{5,13},{9,1},{13,5},{2,10},{6,14},... | collective-permute-start | bytes 1572872 | tf_op jit(solution)/shard_map/ppermute | solution.py:327
  69.0 52.4 %collective-permute-start.2 = (bf16[1024,256]{1,0:T(8,128)(2,1)S(1)}, bf16[1024,256]{1,0:T(8,128)(2,1)S(1)}, u32[]{:S(2)}, u32[]{:S(2)}) collective-permute-start(bf16[1024,256]{1,0:T(8,128)(2,1)S(1)} %get-tuple-element.24), channel_id=1, source_target_pairs={{0,12},{4,0},{8,4},{12,8},{1,13},{5,1},{9,5},{13,9},{2,14},{6,2},{... | collective-permute-start | bytes 1572872 | tf_op jit(solution)/shard_map/ppermute | solution.py:327
  121.4 0.8 copy-start
  121.4 1.0 copy-start.1
  121.4 1.1 copy-start.2

commit v2 on v1

v2 whole, which is shorter than its diff:
```python
import functools
import math
import jax
import jax.numpy as jnp
from jax import lax
from jax.experimental import pallas as pl
from jax.experimental.pallas import tpu as pltpu
from jax.sharding import PartitionSpec as P

DEEP_ALPHA = math.sqrt(140.0)
LN_EPS = 1e-5
ROPE_BASE = 10000.0
MESH = pl.DeviceIdType.MESH
VMEM = pltpu.VMEM
F32 = jnp.float32
BF16 = jnp.bfloat16
N = 4
OTHERS = range(1, N)
HEAD = 64
HALF = HEAD // 2
PART = N * HEAD
PAIR = PART // 2
WIDE = N * PART


def where_am_i():
    dp, x, y = lax.axis_index("dp"), lax.axis_index("x"), lax.axis_index("y")
    core, chip = lax.rem(y, 2), y // 2
    return dp, x, y, core, chip, core * 2 + chip


def remote(src, dst, send, recv, device):
    return pltpu.make_async_remote_copy(
        src_ref=src, dst_ref=dst, send_sem=send, recv_sem=recv, device_id=device, device_id_type=MESH)


def greet(devices):
    barrier = pltpu.get_barrier_semaphore()
    for device in devices:
        pl.semaphore_signal(barrier, inc=1, device_id=device, device_id_type=MESH)
    pl.semaphore_wait(barrier, len(devices))


def qkv_kernel(hid_ref, w_ref, b_ref, bo_ref, ag_ref, as_ref, bd_ref, mg_ref, ms_ref, pos_ref, up_ref, down_ref, wout_ref, vc_ref,
               q_ref, k_ref, v_ref, hres_ref, vecs_ref, p0_ref, p1_ref, p2_ref, p3_ref, vres_ref,
               hbuf, wbuf, vbuf, vrow, acc_ref, cos_ref, sin_ref, hr_s, hl_s, h_r, hy_s, hy_r, hd_s, hd_r, wr_s, wl_s, w_r, wx_s, wx_r, vz_s, vz_r, pre_s):
    dp, x, y, core, chip, piece = where_am_i()
    mate = (dp, x, chip * 2 + 1 - core)
    across = (dp, x, (1 - chip) * 2 + core)
    twin = (1 - dp, x, y)
    peers = [(dp, lax.rem(x + j, N), y) for j in OTHERS]
    source = [lax.rem(x + N - j, N) for j in range(N)]
    right, left = peers[0], peers[2]
    fetch = pltpu.make_async_copy(vc_ref.at[pl.ds(0, RESIDENT)], vres_ref, pre_s)
    fetch.start()
    for n, ref in enumerate((bo_ref, ag_ref, as_ref, bd_ref, mg_ref, ms_ref)):
        vrow[n:n + 1, :] = ref[...].astype(F32).reshape(1, PART)
    vrow[6:8, :] = jnp.zeros((2, 256), F32)
    greet(peers + [mate, across, twin])

    row0 = pl.multiple_of(piece * PART, PART)
    half0 = pl.multiple_of(dp * PAIR, PAIR)
    own_h, own_w = hid_ref.at[pl.ds(row0, 256)], w_ref.at[pl.ds(half0, 128)]

    def h_move(src, s, k, to_right):
        return remote(src, hbuf.at[piece, s], (hr_s if to_right else hl_s).at[k], h_r.at[s], right if to_right else left)

    def w_move(src, s, k, to_right):
        return remote(src, wbuf.at[s, dp], (wr_s if to_right else wl_s).at[k], w_r.at[s], right if to_right else left)

    def y_move(s):
        return remote(hbuf.at[piece, s], hbuf.at[piece, s], hy_s.at[s], hy_r.at[s], across)

    def d_move(s):
        both = hbuf.at[pl.ds(core * 2, 2), s]
        return remote(both, both, hd_s.at[s], hd_r.at[s], mate)

    def x_move(s):
        return remote(wbuf.at[s, dp], wbuf.at[s, dp], wx_s.at[s], wx_r.at[s], twin)

    def sides(k, act):
        @pl.when(x >= k)
        def _():
            act(lax.max(x - k, 0), True)

        @pl.when(x + k <= 3)
        def _():
            act(lax.min(x + k, 3), False)

    def onward(k, act):
        for to_right, at in ((True, x), (False, 3 - x)):
            @pl.when((at - k) * (2 - at) >= 0)
            def _():
                act(lax.max(x - k, 0) if to_right else lax.min(x + k, 3), to_right)

    def start_own(s, to_right):
        h_move(own_h, x, 0, to_right).start()
        w_move(own_w, x, 0, to_right).start()

    def sent_own(s, to_right):
        h_move(own_h, x, 0, to_right).wait_send()
        w_move(own_w, x, 0, to_right).wait_send()

    onward(0, start_own)
    vz = []
    for j in OTHERS:
        c = remote(vrow, vbuf.at[x], vz_s.at[j], vz_r.at[j], peers[j - 1])
        c.start()
        vz.append(c)
    vbuf[x] = vrow[...]
    for part in range(N):
        hbuf[part, x] = hid_ref[part * PART:(part + 1) * PART, :]
    for half in range(2):
        wbuf[x, half] = w_ref[half * PAIR:(half + 1) * PAIR, :]

    for k in OTHERS:
        def arrive_h(s, to_right):
            h_move(hbuf.at[piece, s], s, k, to_right).wait_recv()
            y_move(s).start()

        def arrive_w(s, to_right):
            w_move(wbuf.at[s, dp], s, k, to_right).wait_recv()
            x_move(s).start()

        def arrive_y(s, to_right):
            y_move(s).wait_recv()
            d_move(s).start()

        sides(k, arrive_h)
        if k < 3:
            onward(k, lambda s, to_right: h_move(hbuf.at[piece, s], s, k, to_right).start())
        sides(k, arrive_w)
        if k < 3:
            onward(k, lambda s, to_right: w_move(wbuf.at[s, dp], s, k, to_right).start())
        sides(k, arrive_y)
        if k == 1:
            def own_rows(part, _):
                at = pl.ds(pl.multiple_of(part * PART, PART), 256)
                acc_ref[at, :] = jnp.dot(hid_ref[at, :], w_ref[...], preferred_element_type=F32)
                return 0

            lax.fori_loop(0, N, own_rows, 0)
        if k == 2:
            for j, ref in enumerate((p0_ref, p1_ref, p2_ref, p3_ref)):
                at = pl.ds(pl.multiple_of(lax.rem(x + j, N) * PART, PART), 256)
                ref[0:PART, :] = up_ref[:, 0, at]
                ref[PART:2 * PART, :] = up_ref[:, 1, at]
                ref[2 * PART:3 * PART, :] = down_ref[at, :]
                ref[3 * PART:, :] = wout_ref[...]
            half_dim = lax.broadcasted_iota(jnp.int32, (HALF, WIDE), 0).astype(F32)
            angles = jnp.exp(half_dim * (-2.0 / 64 * math.log(ROPE_BASE))) * pos_ref[...].astype(F32)
            cos_all, sin_all = jnp.cos(angles), jnp.sin(angles)
            cos_ref[...] = cos_all
            sin_ref[...] = sin_all
    far = x // 2
    order = [1 - x + N * far, 2 - far, 3 * (1 - far)]
    for n, s in enumerate(order):
        d_move(s).wait_recv()
        x_move(s).wait_recv()
        vz[n].wait_recv()
        if n < 2:
            def add_rows(part, _):
                at = pl.ds(pl.multiple_of(part * PART, PART), PART)
                acc_ref[at, :] += jnp.dot(hbuf[part, s], wbuf[s].reshape(PART, -1), preferred_element_type=F32)
                return 0

            lax.fori_loop(0, N, add_rows, 0)

    for s in range(N):
        hres_ref[:, s * PART:(s + 1) * PART] = hbuf[x, s, pl.ds(pl.multiple_of(piece * HEAD, HEAD), 64), :]
        vecs_ref[:, s * PART:(s + 1) * PART] = vbuf[s]

    def rows(part, _):
        lanes = pl.ds(pl.multiple_of(part * PART, PART), 256)
        acc = acc_ref[lanes, :]
        acc += jnp.dot(hbuf[part, order[2]], wbuf[order[2]].reshape(PART, -1), preferred_element_type=F32)
        acc = (acc + b_ref[...].astype(F32).reshape(1, -1)).astype(BF16).astype(F32)
        cos, sin = cos_ref[:, lanes], sin_ref[:, lanes]
        acc = acc.T
        for head in range(N):
            base = head * 192
            for off, ref in ((0, q_ref), (64, k_ref)):
                low, high = acc[base + off:base + off + 32], acc[base + off + 32:base + off + 64]
                ref[head * 64:head * 64 + 32, lanes] = (low * cos - high * sin).astype(BF16)
                ref[head * 64 + 32:head * 64 + 64, lanes] = (high * cos + low * sin).astype(BF16)
            v_ref[head * HEAD:(head + 1) * HEAD, lanes] = acc[base + 128:base + 192].astype(BF16)
        return 0

    lax.fori_loop(0, N, rows, 0)
    onward(0, sent_own)
    for k in (1, 2):
        def sent(s, to_right):
            h_move(hbuf.at[piece, s], s, k, to_right).wait_send()
            w_move(wbuf.at[s, dp], s, k, to_right).wait_send()
        onward(k, sent)
    for j in OTHERS:
        vz[j - 1].wait_send()
        y_move(source[j]).wait_send()
        d_move(source[j]).wait_send()
        x_move(source[j]).wait_send()
    fetch.wait()


TILE = 2
DEPTH = 8
ROOM = 44 << 20
RESIDENT = 32


def cache_kernel(len_ref, q_ref, kn_ref, vn_ref, vres_ref, k_ref, v_ref, ko_ref, vo_ref, attn_ref,
                 ibuf, obuf, lens_b, q_own, sc_ref, acc_ref, in_sem, out_sem):
    slots = k_ref.shape[0]
    tiles = slots // TILE
    held = RESIDENT // TILE
    own = pl.ds(pl.multiple_of(lax.axis_index("x") * PART, PART), 256)

    def fetch(ref, t, slot):
        return pltpu.make_async_copy(ref.at[pl.ds(t * TILE, TILE)], ibuf.at[slot], in_sem.at[slot])

    def flush(ref, t, slot):
        return pltpu.make_async_copy(obuf.at[slot], ref.at[pl.ds(t * TILE, TILE)], out_sem.at[slot])

    for t in range(DEPTH):
        fetch(k_ref, t, t).start()
    lens_b[...] = jnp.broadcast_to(len_ref[...].astype(F32), lens_b.shape).astype(BF16)
    q_own[...] = q_ref[:, own].astype(F32)

    def update(slot, i, s, new_ref, old_ref):
        hit = lens_b[...] == jnp.full(lens_b.shape, s.astype(F32), F32).astype(BF16)
        hit = jnp.broadcast_to(hit[None], (16, 16, WIDE))
        old = old_ref[...].reshape(16, 16, WIDE)
        new = new_ref[...].reshape(16, 16, WIDE)
        obuf[slot, i] = jnp.where(hit, new, old).reshape(N, HEAD, WIDE)

    def keys(t, _):
        slot = lax.rem(t, DEPTH)
        fetch(k_ref, t, slot).wait()

        @pl.when(t >= DEPTH)
        def _():
            flush(ko_ref, t - DEPTH, slot).wait()
        for i in range(TILE):
            update(slot, i, t * TILE + i, kn_ref, ibuf.at[slot, i])
        flush(ko_ref, t, slot).start()

        @pl.when(t < tiles - DEPTH)
        def _():
            fetch(k_ref, t + DEPTH, slot).start()

        @pl.when(t >= tiles - DEPTH)
        def _():
            fetch(v_ref, held + t + DEPTH - tiles, slot).start()
        for i in range(TILE):
            for head in range(N):
                prod = obuf[slot, i, head, :, own].astype(F32) * q_own[head * HEAD:(head + 1) * HEAD, :]
                sc_ref[head, pl.ds(t * TILE + i, 1), :] = jnp.sum(prod, axis=0, keepdims=True)
        return 0

    lax.fori_loop(0, tiles, keys, 0)
    sc = sc_ref[...] * (HEAD ** -0.5)
    valid = lax.broadcasted_iota(jnp.int32, sc.shape, 1) <= jnp.broadcast_to(len_ref[:, own][None], sc.shape)
    sc = jnp.where(valid, sc, -1e30)
    e = jnp.exp(sc - jnp.max(sc, axis=1, keepdims=True))
    sc_ref[...] = (e / jnp.sum(e, axis=1, keepdims=True)).astype(BF16).astype(F32)
    acc_ref[...] = jnp.zeros_like(acc_ref)

    def weigh(slot, t):
        for head in range(N):
            at = slice(head * HEAD, (head + 1) * HEAD)
            part = acc_ref[at, :]
            for i in range(TILE):
                part += obuf[slot, i, head, :, own].astype(F32) * sc_ref[head, pl.ds(t * TILE + i, 1), :]
            acc_ref[at, :] = part

    def values(n, _):
        slot, t = lax.rem(n, DEPTH), held + n
        fetch(v_ref, t, slot).wait()

        @pl.when(n >= DEPTH)
        def _():
            flush(vo_ref, t - DEPTH, slot).wait()

        @pl.when(n < DEPTH)
        def _():
            flush(ko_ref, n + tiles - DEPTH, slot).wait()
        for i in range(TILE):
            update(slot, i, t * TILE + i, vn_ref, ibuf.at[slot, i])
        flush(vo_ref, t, slot).start()

        @pl.when(n < tiles - held - DEPTH)
        def _():
            fetch(v_ref, t + DEPTH, slot).start()
        weigh(slot, t)
        return 0

    def held_values(t, _):
        slot = lax.rem(t, DEPTH)
        flush(vo_ref, t, slot).wait()
        for i in range(TILE):
            update(slot, i, t * TILE + i, vn_ref, vres_ref.at[t * TILE + i])
        flush(vo_ref, t, slot).start()
        weigh(slot, t)
        return 0

    lax.fori_loop(0, tiles - held, values, 0)
    lax.fori_loop(0, held, held_values, 0)
    attn_ref[...] = acc_ref[...].astype(BF16)
    for slot in range(DEPTH):
        flush(vo_ref, slot, slot).wait()


def whole_row_norm(h, gain, shift):
    mean = jnp.mean(h, axis=-1, keepdims=True)
    dev = h - mean
    var = jnp.mean(dev * dev, axis=-1, keepdims=True)
    return (dev * lax.rsqrt(var + LN_EPS) * gain + shift).astype(BF16)


def mlp_kernel(attn_ref, w0_ref, w1_ref, w2_ref, w3_ref, hres_ref, vecs_ref, bup_ref,
               out_ref,
               wg, wv, wd, wo, p1, s1d, r1d, s1y, r1y, zfull,
               keep, sd, rd, sy, ry, sz, rz, ob, ofull,
               a_s, a_r, zz_s, zz_r, zy_s, zy_r, zd_s, zd_r,
               md_s, md_r, my_s, my_r, mz_s, mz_r, oz_s, oz_r, oy_s, oy_r, od_s, od_r):
    dp, x, y, core, chip, piece = where_am_i()
    mate = (dp, x, chip * 2 + 1 - core)
    across = (dp, x, (1 - chip) * 2 + core)
    peers = [(dp, lax.rem(x + j, N), y) for j in OTHERS]
    source = [lax.rem(x + N - j, N) for j in range(N)]
    sends = []

    def go(src, dst, send, recv, device):
        c = remote(src, dst, send, recv, device)
        c.start()
        sends.append(c)
        return c

    greet(peers + [mate, across])
    bup = bup_ref[:, pl.ds(pl.multiple_of(x * PART, PART), 256)].astype(F32)
    columns = [pl.ds(pl.multiple_of(source[j] * PART, PART), 256) for j in range(N)]
    packs = (w0_ref, w1_ref, w2_ref, w3_ref)
    for j in range(N):
        wo[:, columns[j]] = packs[j][3 * PART:, :]

    mine = attn_ref[...].astype(F32).T.astype(BF16)
    p1[...] = jnp.dot(mine, wo[...], preferred_element_type=F32)
    s1d[...] = p1[pl.ds(pl.multiple_of((1 - core) * PAIR, PAIR), 128), :].astype(BF16)
    c = go(s1d, r1d, a_s.at[0], a_r.at[0], mate)
    for j in range(N):
        wd[:, columns[j]] = packs[j][2 * PART:3 * PART, :]
    c.wait_recv()
    give = (1 - chip) * 64
    hold = chip * 64
    base = core * 128
    s1y[...] = (p1[pl.ds(pl.multiple_of(base + give, HEAD), HEAD), :]
                + r1d[pl.ds(pl.multiple_of(give, HEAD), HEAD), :].astype(F32)).astype(BF16)
    c = go(s1y, r1y, a_s.at[1], a_r.at[1], across)
    h = (p1[pl.ds(pl.multiple_of(base + hold, HEAD), HEAD), :]
         + r1d[pl.ds(pl.multiple_of(hold, HEAD), HEAD), :].astype(F32))
    for j in range(N):
        wg[columns[j], :] = packs[j][0:PART, :]
        wv[columns[j], :] = packs[j][PART:2 * PART, :]
    c.wait_recv()
    h = h + r1y[...].astype(F32)
    h = DEEP_ALPHA * hres_ref[...].astype(F32) + (h + vecs_ref[0:1, :])
    zfull[x, piece] = whole_row_norm(h, vecs_ref[1:2, :], vecs_ref[2:3, :])

    own = zfull.at[x, piece]
    zz = [go(own, own, zz_s.at[j], zz_r.at[j], peers[j - 1]) for j in OTHERS]
    zy = [go(own, own, zy_s.at[0], zy_r.at[0], across)]
    for j in OTHERS:
        zz[j - 1].wait_recv()
        block = zfull.at[source[j], piece]
        zy.append(go(block, block, zy_s.at[j], zy_r.at[j], across))
        if j == 1:
            zy[0].wait_recv()
            both = zfull.at[x, pl.ds(core * 2, 2)]
            zd = [go(both, both, zd_s.at[0], zd_r.at[0], mate)]

    def mlp(j):
        z = zfull[source[j]].reshape(PART, WIDE)
        gate = jnp.dot(z, wg[...], preferred_element_type=F32) + bup[0:1, :]
        value = jnp.dot(z, wv[...], preferred_element_type=F32) + bup[1:2, :]
        g = (jax.nn.gelu(gate, approximate=True) * value).astype(BF16)
        p1[...] = jnp.dot(g, wd[...], preferred_element_type=F32)
        sd[j] = p1[pl.ds(pl.multiple_of((1 - core) * PAIR, PAIR), 128), :].astype(BF16)
        keep[j] = p1[pl.ds(pl.multiple_of(base, 128), 128), :]
        return go(sd.at[j], rd.at[j], md_s.at[j], md_r.at[j], mate)

    def pair_sum(j, c):
        c.wait_recv()
        at = pl.ds(pl.multiple_of(give, HEAD), HEAD)
        sy[j] = (keep[j, at, :] + rd[j, at, :].astype(F32)).astype(BF16)
        return go(sy.at[j], ry.at[j], my_s.at[j], my_r.at[j], across)

    def chip_sum(j, c):
        c.wait_recv()
        at = pl.ds(pl.multiple_of(hold, HEAD), HEAD)
        total = keep[j, at, :] + rd[j, at, :].astype(F32) + ry[j].astype(F32)
        if j == 0:
            keep[0, 0:64, :] = total
            return None
        sz[j] = total.astype(BF16)
        back = (dp, source[j], y)
        return go(sz.at[j], rz.at[j], mz_s.at[j], mz_r.at[j], back)

    my, mz = {}, {}
    for t in range(N):
        zd[t].wait_recv()
        c = mlp(t)
        if t < 3:
            zy[t + 1].wait_recv()
            both = zfull.at[source[t + 1], pl.ds(core * 2, 2)]
            zd.append(go(both, both, zd_s.at[t + 1], zd_r.at[t + 1], mate))
        my[t] = pair_sum(t, c)
        if t > 0:
            mz[t - 1] = chip_sum(t - 1, my[t - 1])
    mz[3] = chip_sum(3, my[3])
    h = keep[0, 0:64, :]
    for j in OTHERS:
        mz[j].wait_recv()
        h = h + rz[j].astype(F32)
    h = DEEP_ALPHA * zfull[x, piece].astype(F32) + h + vecs_ref[3:4, :]
    o = whole_row_norm(h, vecs_ref[4:5, :], vecs_ref[5:6, :])

    for s in range(N):
        ob[s] = o[:, s * PART:(s + 1) * PART]
    ofull[x, piece] = ob[x]
    oz = [go(ob.at[lax.rem(x + j, N)], ofull.at[x, piece], oz_s.at[j], oz_r.at[j], peers[j - 1]) for j in OTHERS]
    oy = []
    for j in range(N):
        if j > 0:
            oz[j - 1].wait_recv()
        block = ofull.at[source[j], piece]
        oy.append(go(block, block, oy_s.at[j], oy_r.at[j], across))
    od = []
    for j in range(N):
        oy[j].wait_recv()
        both = ofull.at[source[j], pl.ds(core * 2, 2)]
        od.append(go(both, both, od_s.at[j], od_r.at[j], mate))
    for c in od:
        c.wait_recv()
    out_ref[...] = ofull[...].reshape(WIDE, PART)
    for c in sends:
        c.wait_send()


def solution(mesh):
    cache_spec = P('dp', None, 'y', None)
    width_spec = P('x')
    in_specs = (P('dp', 'x'), P('x', 'y'), P('y'), P('y', 'x'), width_spec, width_spec, width_spec, P('x', None, 'y'), P(None, 'y'), P('y', 'x'), width_spec, width_spec, width_spec, cache_spec, cache_spec, P('dp'), P('dp'))
    out_specs = (P('dp', 'x'), cache_spec, cache_spec)
    vmem = pl.BlockSpec(memory_space=VMEM)
    dma = pltpu.SemaphoreType.DMA

    def local_step(hidden, w_qkv, b_qkv, w_out, b_out, attn_gain, attn_shift, w_up, b_up, w_down, b_down, mlp_gain, mlp_shift, k_cache, v_cache, positions, lengths):
        k_t, v_t = k_cache.transpose(1, 2, 3, 0), v_cache.transpose(1, 2, 3, 0)
        anywhere = pl.BlockSpec(memory_space=pl.ANY)
        row = jax.ShapeDtypeStruct((PART, WIDE), BF16)
        pack = jax.ShapeDtypeStruct((WIDE, PART), BF16)
        q, k_new, v_new, hres, vecs, *packs, v_res = pl.pallas_call(
            qkv_kernel,
            name="gather_qkv",
            out_shape=(row, row, row, jax.ShapeDtypeStruct((HEAD, WIDE), BF16), jax.ShapeDtypeStruct((8, WIDE), F32)) + (pack,) * 4 + (VMEM((RESIDENT, N, HEAD, WIDE), BF16),),
            in_specs=[vmem] * 13 + [anywhere],
            out_specs=(vmem,) * 10,
            scratch_shapes=[
                VMEM((N, N, PART, PART), BF16),
                VMEM((4, 2, 128, 768), BF16),
                VMEM((N, 8, PART), F32),
                VMEM((8, PART), F32),
                VMEM((1024, 768), F32),
                VMEM((HALF, WIDE), F32),
                VMEM((HALF, WIDE), F32),
            ] + [dma((N,))] * 14 + [dma(())],
            compiler_params=pltpu.CompilerParams(collective_id=0, has_side_effects=True, vmem_limit_bytes=ROOM),
            cost_estimate=pl.CostEstimate(flops=2 * 1024 * 1024 * 768, bytes_accessed=8 << 20, transcendentals=0),
        )(hidden, w_qkv, b_qkv, b_out, attn_gain, attn_shift, b_down, mlp_gain, mlp_shift, positions.reshape(1, WIDE), w_up, w_down, w_out, v_t)

        moved = [packs[0]] + [lax.ppermute(packs[j], 'x', [(i, (i + j) % 4) for i in range(N)]) for j in OTHERS]

        k_full, v_full, attn = pl.pallas_call(
            cache_kernel,
            name="cache_attend",
            out_shape=(jax.ShapeDtypeStruct(k_t.shape, BF16), jax.ShapeDtypeStruct(v_t.shape, BF16), jax.ShapeDtypeStruct((PART, PART), BF16)),
            in_specs=[vmem] * 5 + [anywhere] * 2,
            out_specs=(anywhere, anywhere, vmem),
            scratch_shapes=[
                VMEM((DEPTH, TILE, N, HEAD, WIDE), BF16), VMEM((DEPTH, TILE, N, HEAD, WIDE), BF16),
                VMEM((16, 1024), BF16), VMEM((PART, PART), F32), VMEM((N, HEAD, PART), F32), VMEM((PART, PART), F32),
                dma((DEPTH,)), dma((DEPTH,)),
            ],
            compiler_params=pltpu.CompilerParams(vmem_limit_bytes=ROOM),
            cost_estimate=pl.CostEstimate(flops=4 * 10 ** 9, bytes_accessed=128 << 20, transcendentals=0),
        )(lengths.reshape(1, WIDE), q, k_new, v_new, pltpu.with_memory_space_constraint(v_res, VMEM), k_t, v_t)

        out = pl.pallas_call(
            mlp_kernel,
            name="project_mlp",
            out_shape=jax.ShapeDtypeStruct((WIDE, PART), BF16),
            in_specs=[vmem] * 8,
            out_specs=vmem,
            scratch_shapes=[
                VMEM((WIDE, PART), BF16), VMEM((WIDE, PART), BF16), VMEM((PART, WIDE), BF16), VMEM((PART, WIDE), BF16),
                VMEM((PART, WIDE), F32),
                VMEM((PAIR, WIDE), BF16), VMEM((PAIR, WIDE), BF16), VMEM((HEAD, WIDE), BF16), VMEM((HEAD, WIDE), BF16),
                VMEM((N, N, HEAD, WIDE), BF16),
                VMEM((N, PAIR, WIDE), F32),
                VMEM((N, PAIR, WIDE), BF16), VMEM((N, PAIR, WIDE), BF16),
                VMEM((N, HEAD, WIDE), BF16), VMEM((N, HEAD, WIDE), BF16),
                VMEM((N, HEAD, WIDE), BF16), VMEM((N, HEAD, WIDE), BF16),
                VMEM((N, HEAD, PART), BF16),
                VMEM((N, N, HEAD, PART), BF16),
            ] + [dma((N,))] * 20,
            compiler_params=pltpu.CompilerParams(collective_id=1, has_side_effects=True, vmem_limit_bytes=ROOM),
            cost_estimate=pl.CostEstimate(flops=4 * 10 ** 9, bytes_accessed=8 << 20, transcendentals=0),
        )(attn, *moved, hres, vecs, b_up)
        return out, k_full.transpose(3, 0, 1, 2), v_full.transpose(3, 0, 1, 2)

    return jax.shard_map(local_step, mesh=mesh, in_specs=in_specs, out_specs=out_specs, check_vma=False)
```

time: 182 us -> 142 us (0.78)
  Pallas kernels: 153 us -> 136 us
  local copies, waits for them, and re-layouts: 13.6 us -> 1.71 us
  other arithmetic: 5.63 us -> 0 us
  starting transfers between devices: 8.95 us -> 3.87 us
    pallas_call x1, Pallas kernels: 49.8 us -> 39.8 us  [local_step(): pl.pallas_call(cache_kernel, name='cache_attend', out_shape=(jax.ShapeDty...]
    pallas_call x1, Pallas kernels: 45.7 us -> 39 us  [local_step(): pl.pallas_call(qkv_kernel, name='gather_qkv', out_shape=(row, row, row, j...]
    ppermute x3, starting transfers between devices: 8.95 us -> 3.87 us  [local_step(): lax.ppermute(packs[j], 'x', [(i, (i + j) % 4) for i in range(N)])]
    slice x1 -> x0, local copies, waits for them, and re-layouts: 4.06 us -> none  [local_step(): packs.append(jnp.concatenate([up[:, 0], up[:, 1], down, w_out], axis=0))]
    another operation x7 -> x0, local copies, waits for them, and re-layouts: 3.98 us -> none  [local_step(): jnp.stack([v.astype(F32) for v in (b_out, attn_gain, attn_shift, b_down,...]
    convert_element_type x2 -> x0, other arithmetic: 1.95 us -> none  [the longest x1 1.25 us: local_step(): bup = lax.dynamic_slice_in_dim(b_up, x * 256, 256, axis=1).astype(F32)]
    concatenate x1 -> x0, other arithmetic: 1.83 us -> none  [local_step(): packs.append(jnp.concatenate([up[:, 0], up[:, 1], down, w_out], axis=0))]
  transfers between devices with their start and end apart: 3 -> 3, of which waited for: 0 -> 0; matrix products, arithmetic and copies ran while one was open for 1% -> 0% of each run, Pallas kernels for 27% -> 28%
where the time goes in v2:
time: 142 us
  Pallas kernels  136 us (96%)
  starting transfers between devices  3.87 us (3%)
  local copies, waits for them, and re-layouts  1.71 us (1%)
    pallas_call x1, Pallas kernels, local_step(): pl.pallas_call(mlp_kernel, name='project_mlp', out_shape=jax.ShapeDtypeSt...  57 us
    pallas_call x1, Pallas kernels, local_step(): pl.pallas_call(cache_kernel, name='cache_attend', out_shape=(jax.ShapeDty...  39.8 us
    pallas_call x1, Pallas kernels, local_step(): pl.pallas_call(qkv_kernel, name='gather_qkv', out_shape=(row, row, row, j...  39 us
    ppermute x3, starting transfers between devices, local_step(): lax.ppermute(packs[j], 'x', [(i, (i + j) % 4) for i in range(N)])  3.87 us
  transfers between devices with their start and end apart: 3, of which 0 were waited for; matrix products, arithmetic and copies ran while one was open for 0% of the time, Pallas kernels for 28%

profile of v2, /device:TPU:0, one launch (start us, length us, event | category | flops | bytes accessed | tf_op | source)
XLA Modules:
  0.0 142.1 jit_solution(637677821482987493)
XLA Ops:
  0.6 39.0 %gather_qkv.1 = (bf16[256,1024]{1,0:T(8,128)(2,1)}, bf16[256,1024]{1,0:T(8,128)(2,1)}, bf16[256,1024]{1,0:T(8,128)(2,1)}, bf16[64,1024]{1,0:T(8,128)(2,1)}, f32[...) custom-call(bf16[1024,256]{1,0:T(8,128)(2,1)} %hid_ref.1, ...), custom_call_target="tpu_custom_call" | custom-call | flops 1610612736 | bytes 8388608 | tf_op jit(solution)/shard_map/gather_qkv/pallas_call | solution.py:461
  39.6 0.1 collective-permute-start
  39.7 2.0 %collective-permute-start.1 = (bf16[1024,256]{1,0:T(8,128)(2,1)}, bf16[1024,256]{1,0:T(8,128)(2,1)S(1)}, u32[]{:S(2)}, u32[]{:S(2)}) collective-permute-start(bf16[1024,256]{1,0:T(8,128)(2,1)} %get-tuple-element.23), channel_id=1, source_target_pairs={{0,8},{4,12},{8,0},{12,4},{1,9},{5,13},{9,1},{13,5},{2,10},{6,14},... | collective-permute-start | bytes 1572872 | tf_op jit(solution)/shard_map/ppermute | solution.py:480
  41.7 1.8 %collective-permute-start.2 = (bf16[1024,256]{1,0:T(8,128)(2,1)}, bf16[1024,256]{1,0:T(8,128)(2,1)S(1)}, u32[]{:S(2)}, u32[]{:S(2)}) collective-permute-start(bf16[1024,256]{1,0:T(8,128)(2,1)} %get-tuple-element.24), channel_id=1, source_target_pairs={{0,12},{4,0},{8,4},{12,8},{1,13},{5,1},{9,5},{13,9},{2,14},{6,2},{... | collective-permute-start | bytes 1572872 | tf_op jit(solution)/shard_map/ppermute | solution.py:480
  43.5 0.0 copy-start
  43.5 0.0 copy-start.1
  43.5 0.0 copy-start.3
  43.5 0.0 copy-start.4
  43.5 39.8 %cache_attend.1 = (bf16[64,4,64,1024]{3,2,1,0:T(8,128)(2,1)}, bf16[64,4,64,1024]{3,2,1,0:T(8,128)(2,1)}, bf16[256,256]{1,0:T(8,128)(2,1)}) custom-call(s32[1,1024]{1,0:T(1,128)} %bitcast.10, bf16[256,1024]{1,0:T(8,128)(2,1)} %get-tuple-element.16.q_ref, bf16[256,1024]{1,0:T(8,128)(2,1)} %get-tuple-element.17.kn_ref, ...), custom_call_target="tpu_custom_call" | custom-call | flops 4000000000 | bytes 134217728 | tf_op jit(solution)/shard_map/cache_attend/pallas_call | solution.py:482
  83.3 0.0 collective-permute-done.w1_ref
  83.3 0.0 collective-permute-done.1.w2_ref
  83.3 0.0 collective-permute-done.2.w3_ref
  83.4 0.0 copy-done
  83.4 0.0 copy-done.1
  83.4 0.0 copy-done.3
  83.4 0.0 copy-done.4
  83.4 0.0 copy-start.2
  83.4 0.9 copy-done.2
  84.3 57.0 %project_mlp.1 = bf16[1024,256]{1,0:T(8,128)(2,1)S(1)} custom-call(bf16[256,256]{1,0:T(8,128)(2,1)S(1)} %copy-done.2, bf16[1024,256]{1,0:T(8,128)(2,1)S(1)} %copy-done, bf16[1024,256]{1,0:T(8,128)(2,1)S(1)} %collective-permute-done.w1_ref, bf16[1024,256]{1,0:T(8,128)(2,1)S(1)} %collective-permute-done.1.w2_ref, ...), custom_call_target="tpu_custom_call" | custom-call | flops 4000000000 | bytes 8388608 | tf_op jit(solution)/shard_map/project_mlp/pallas_call | solution.py:497
  141.3 0.8 copy.21
Async XLA Ops:
  39.6 43.7 %collective-permute-start = (bf16[1024,256]{1,0:T(8,128)(2,1)}, bf16[1024,256]{1,0:T(8,128)(2,1)S(1)}, u32[]{:S(2)}, u32[]{:S(2)}) collective-permute-start(bf16[1024,256]{1,0:T(8,128)(2,1)} %get-tuple-element.22), channel_id=1, source_target_pairs={{0,4},{4,8},{8,12},{12,0},{1,5},{5,9},{9,13},{13,1},{2,6},{6,10},{... | collective-permute-start | bytes 1572872 | tf_op jit(solution)/shard_map/ppermute | solution.py:480
  39.7 43.6 %collective-permute-start.1 = (bf16[1024,256]{1,0:T(8,128)(2,1)}, bf16[1024,256]{1,0:T(8,128)(2,1)S(1)}, u32[]{:S(2)}, u32[]{:S(2)}) collective-permute-start(bf16[1024,256]{1,0:T(8,128)(2,1)} %get-tuple-element.23), channel_id=1, source_target_pairs={{0,8},{4,12},{8,0},{12,4},{1,9},{5,13},{9,1},{13,5},{2,10},{6,14},... | collective-permute-start | bytes 1572872 | tf_op jit(solution)/shard_map/ppermute | solution.py:480
  41.7 41.7 %collective-permute-start.2 = (bf16[1024,256]{1,0:T(8,128)(2,1)}, bf16[1024,256]{1,0:T(8,128)(2,1)S(1)}, u32[]{:S(2)}, u32[]{:S(2)}) collective-permute-start(bf16[1024,256]{1,0:T(8,128)(2,1)} %get-tuple-element.24), channel_id=1, source_target_pairs={{0,12},{4,0},{8,4},{12,8},{1,13},{5,1},{9,5},{13,9},{2,14},{6,2},{... | collective-permute-start | bytes 1572872 | tf_op jit(solution)/shard_map/ppermute | solution.py:480
  43.5 39.9 %copy-start = (bf16[1024,256]{1,0:T(8,128)(2,1)S(1)}, bf16[1024,256]{1,0:T(8,128)(2,1)}, u32[]{:S(2)}) copy-start(bf16[1024,256]{1,0:T(8,128)(2,1)} %get-tuple-element.21.w0_ref) | copy-start | bytes 1572868
  43.5 39.9 %copy-start.1 = (bf16[64,1024]{1,0:T(8,128)(2,1)S(1)}, bf16[64,1024]{1,0:T(8,128)(2,1)}, u32[]{:S(2)}) copy-start(bf16[64,1024]{1,0:T(8,128)(2,1)} %get-tuple-element.25.hres_ref) | copy-start | bytes 393220
  43.5 39.9 %copy-start.3 = (f32[8,1024]{1,0:T(8,128)S(1)}, f32[8,1024]{1,0:T(8,128)}, u32[]{:S(2)}) copy-start(f32[8,1024]{1,0:T(8,128)} %get-tuple-element.26.vecs_ref) | copy-start | bytes 98308
  43.5 39.9 %copy-start.4 = (bf16[2,1024]{1,0:T(2,128)(2,1)S(1)}, bf16[2,1024]{1,0:T(2,128)(2,1)}, u32[]{:S(2)}) copy-start(bf16[2,1024]{1,0:T(2,128)(2,1)} %bup_ref.1) | copy-start | bytes 12292
  83.4 0.9 copy-start.2
